TPU v7x, 32 devices: a whole 2x2x4 slice. The times are simulated.
32 devices in a mesh: seq: 8 (over y, x, core), head: 4 (over z).
Axes of the slice: x: 2, y: 2, z: 4, core: 2. Of those that a mesh axis runs over, the one named last changes fastest.
Arguments:
- values: bfloat16 [16384, 5120], P('seq', 'head'), may hold values from -6 to 6
- gates: bfloat16 [16384, 5120], P('seq', 'head'), may hold values from -6 to 6
- b_proj: bfloat16 [16384, 128], P('seq'), may hold values from -2 to 2
- c_proj: bfloat16 [16384, 128], P('seq'), may hold values from -2 to 2
- step_size: float32 [80, 16384], P('head', 'seq'), may hold values from 0.006 to 0.06
- decay_rate: float32 [80, 16384], P('head', 'seq'), may hold values from 0 to 1.2, as said below
- skip_gain: float32 [80], P('head'), may hold values from 0.5 to 2
- norm_gain: float32 [5120], P('head'), may hold values from 0.25 to 1.75
- readout_matrix: bfloat16 [5120, 2560], P('head'), may hold values from -0.078125 to 0.078125
- span_counts: int32 [8], P('seq'), may hold values from 1 to 8, as said below
- remaining_count: int32 [8], P('seq'), may hold values from 1 to 256
Outputs:
- mixer_response: bfloat16 [16384, 2560], P(('seq', 'head'))
Inputs may be any that keep to these rules, and one draw needn't show every extreme that they name: `span_counts`: some shard uses all 8 span slots in every draw. `decay_rate`: Positive.
All inputs are finite; a program needn't handle non-finite values.
Results may differ from a plain program's by a relative error of at most 0.02.
Values may be sent and summed in bfloat16 or wider, within the bound.
A program may use at most 192 MiB of HBM per device.

v0:
```python
import jax
import jax.numpy as jnp
from jax import lax
from jax.sharding import PartitionSpec as P

HEADS = 80
P_SIZE = 64
SPAN = 256


def prefix_2(value, axis, combine, identity):
    count, place = (lax.axis_size(axis), lax.axis_index(axis))
    everything = jax.tree.map(
        lambda part, kind: lax.all_gather(part.astype(kind), axis),
        value,
        (jnp.bfloat16, jnp.bfloat16),
    )
    start = jax.tree.map(
        lambda part, zero: jnp.broadcast_to(jnp.asarray(zero, part.dtype), part.shape),
        value,
        identity,
    )

    def lap(k, before):
        reached = k < place
        new = combine(
            before, jax.tree.map(lambda part, own: part[k].astype(own.dtype), everything, value)
        )
        return jax.tree.map(lambda a, b: jnp.where(reached, a, b), new, before)

    return lax.fori_loop(0, count, lap, start)


def body(
    values,
    gates,
    b_proj,
    c_proj,
    step_size,
    decay_rate,
    skip_gain,
    norm_gain,
    readout_matrix,
    span_counts,
    remaining_count,
):
    f32 = jnp.float32
    bf16 = jnp.bfloat16
    length = values.shape[0]
    heads = step_size.shape[0]
    head_dim = values.shape[1] // heads
    state_list = b_proj.shape[1]
    blocks = length // SPAN
    valid = (span_counts[0] - 1) * SPAN + remaining_count[0]
    live = (jnp.arange(length, dtype=jnp.int32) < valid).astype(f32)
    logdec = (-decay_rate * live[None, :]).reshape(heads, blocks, SPAN)
    running = jnp.cumsum(logdec, axis=2)
    weight = (step_size * live[None, :]).reshape(heads, blocks, SPAN)
    heads_x = values.reshape(blocks, SPAN, heads, head_dim)
    c_blocks = c_proj.reshape(blocks, SPAN, state_list)
    b_blocks = b_proj.reshape(blocks, SPAN, state_list)
    gram = jnp.einsum("cin,cjn->cij", c_blocks, b_blocks, preferred_element_type=f32)
    lower = jnp.arange(SPAN)[:, None] >= jnp.arange(SPAN)[None, :]
    spread = jnp.where(lower, running[..., :, None] - running[..., None, :], -1e30)
    mixing = (gram[None] * jnp.exp(spread) * weight[:, :, None, :]).astype(bf16)
    inner = jnp.einsum("hcij,cjhp->cihp", mixing, heads_x, preferred_element_type=f32)
    tail = jnp.exp(running[..., -1:] - running) * weight
    weighted = (heads_x * tail.transpose(1, 2, 0)[..., None]).astype(bf16)
    fresh = jnp.einsum("cjhp,cjn->chpn", weighted, b_blocks, preferred_element_type=f32)
    block_decay = running[..., -1]

    def shard_step(state, item):
        decay, piece = item
        return (jnp.exp(decay)[:, None, None] * state + piece, state)

    empty = jnp.zeros((heads, head_dim, state_list), f32)
    shard_state, before = lax.scan(shard_step, empty, (block_decay.T, fresh))
    dev_decay = jnp.sum(block_decay, axis=1)

    def join(earlier, later):
        return (earlier[0] + later[0], jnp.exp(later[0])[:, None, None] * earlier[1] + later[1])

    prefix = prefix_2((dev_decay, shard_state), "seq", join, (jnp.zeros_like(dev_decay), empty))
    incoming = prefix[1]
    leading = jnp.cumsum(block_decay, axis=1) - block_decay
    entering = before + jnp.exp(leading.T)[:, :, None, None] * incoming[None]
    carried = jnp.einsum(
        "cin,chpn->cihp", c_blocks, entering.astype(bf16), preferred_element_type=f32
    )
    carried = carried * jnp.exp(running).transpose(1, 2, 0)[..., None]
    mixed = (inner + carried + skip_gain[None, None, :, None] * heads_x) * live.reshape(
        blocks, SPAN
    )[:, :, None, None]
    gated = mixed.reshape(length, heads * head_dim) * jax.nn.silu(gates.astype(f32))
    squares = lax.psum(jnp.sum(gated * gated, axis=1), "head")
    normed = (
        gated * lax.rsqrt(squares / (HEADS * P_SIZE) + 1e-05)[:, None] * norm_gain[None, :]
    ).astype(bf16)
    summed = lax.psum_scatter(
        jnp.dot(normed, readout_matrix, preferred_element_type=f32).astype(jnp.bfloat16),
        "head",
        scatter_dimension=0,
        tiled=True,
    ).astype(jnp.float32)
    return summed.astype(bf16)


def solution(mesh):
    return jax.shard_map(
        body,
        mesh=mesh,
        in_specs=(
            P("seq", "head"),
            P("seq", "head"),
            P("seq", None),
            P("seq", None),
            P("head", "seq"),
            P("head", "seq"),
            P("head"),
            P("head"),
            P("head", None),
            P("seq"),
            P("seq"),
        ),
        out_specs=P(("seq", "head"), None),
        check_vma=False,
    )
```

profile of v0, /device:TPU:0, one launch (start us, length us, event | category | flops | bytes accessed | tf_op | source)
XLA Modules:
  0.0 370.2 jit_solution(3771847295021560129)
XLA Ops:
  9.1 11.3 %reduce-window.6 = f32[20,8,2,128]{3,1,2,0:T(8,128)S(1)} reduce-window(f32[20,8,2,128]{3,1,2,0:T(8,128)S(1)} %copy.48, f32[]{:T(128)} %constant.61.clone.1), window={size=1x1x1x128 pad=0_0x0_0x0_0x127_0}, to_apply=%region_0.0 | reduce-window | flops 5201920 | bytes 327684 | tf_op jit(solution)/shard_map/reduce-window
  21.9 8.0 %copy.54 = bf16[2048,1280]{0,1:T(8,128)(2,1)} copy(bf16[2048,1280]{1,0:T(8,128)(2,1)} %param.15) | data formatting | bytes 10485760 | tf_op args[0]
  29.9 7.1 %copy.67 = bf16[160,8,8,256]{3,2,1,0:T(8,128)(2,1)} copy(bf16[160,8,8,256]{3,1,2,0:T(8,128)(2,1)} %bitcast.85) | data formatting | bytes 10485760
  37.0 6.3 %fusion.18 = f32[8,20,64,128]{3,2,1,0:T(8,128)} fusion(bf16[8,256,128,1]{2,1,3,0:T(8,128)(2,1)S(1)} %bitcast.89, f32[8,256,20]{1,2,0:T(8,128)S(1)} %copy.59, bf16[8,256,20,64]{1,0,3,2:T(8,128)(2,1)} %bitcast.82), kind=kOutput, calls=%fused_computation.32 | convolution fusion | flops 678952960 | bytes 11173888 | tf_op jit(solution)/shard_map/cjhp,cjn->chpn/dot_general | solution.py:69
  43.4 17.2 %while.27 = (s32[]{:T(128)}, f32[20,64,128]{2,1,0:T(8,128)S(1)}, f32[8,20,64,128]{3,2,1,0:T(8,128)}, f32[8,20]{1,0:T(8,128)S(1)}, f32[8,20,64,128]{3,2,1,0:T(8,128)}, /*index=5*/s32[]{:T(128)}, s32[]{:T(128)}) while((s32[]{:T(128)}, f32[20,64,128]{2,1,0:T(8,128)S(1)}, f32[8,20,64,128]{3,2,1,0:T(8,128)}, f32[8,20]{1,0:T(8,128)S(1)}, ...), condition=%wide.region_3.4_spmd.clone, body=%wide.region_2.3_spmd.clone.sunk | while | flops 655363 | bytes 3277648 | solution.py:77
  44.3 1.2 bitcast_add_fusion.2
  46.4 1.2 bitcast_add_fusion.2
  48.6 1.2 bitcast_add_fusion.2
  50.7 1.2 bitcast_add_fusion.2
  52.9 1.2 bitcast_add_fusion.2
  55.0 1.2 bitcast_add_fusion.2
  57.2 1.2 bitcast_add_fusion.2
  63.1 15.6 %all-reduce = bf16[160]{0:T(256)(128)(2,1)S(1)} all-reduce(bf16[160]{0:T(256)(128)(2,1)S(1)} %dynamic-update-slice), channel_id=2, replica_groups=mesh['seq'=8,'head'=4] {'seq'}, use_global_device_ids=true, to_apply=%add | all-reduce | flops 160 | bytes 640
  78.9 8.2 %copy.62 = bf16[2048,1280]{0,1:T(8,128)(2,1)} copy(bf16[2048,1280]{1,0:T(8,128)(2,1)} %param.16) | data formatting | bytes 10485760 | tf_op args[1]
  87.5 16.5 %fusion.3 = f32[8,20,256,64]{2,3,1,0:T(8,128)} fusion(f32[20,8,256]{2,0,1:T(8,128)S(1)} %copy.53, f32[20,8,256]{2,0,1:T(8,128)S(1)} %copy.51, f32[8,256,256]{2,1,0:T(8,128)S(1)} %fusion.33, pred[256,256]{1,0:T(8,128)(4,1)S(1)} %iota_compare_fusion, bf16[8,256,20,64]{1,0,3,2:T(8,128)(2,1)} %bitcast.83), kind=kOutput, calls=%fused_computation.9 | convolution fusion | flops 1394606080 | bytes 18219008 | tf_op jit(solution)/shard_map/hcij,cjhp->cihp/dot_general | solution.py:66
  104.0 9.4 %while.28 = (s32[]{:T(128)}, f32[20,64,128]{2,1,0:T(8,128)S(1)}, s32[]{:T(128)}, bf16[8,20]{1,0:T(8,128)(2,1)S(1)}, bf16[8,20,64,128]{3,2,1,0:T(8,128)(2,1)}, /*index=5*/s32[]{:T(128)}, s32[]{:T(128)}) while((s32[]{:T(128)}, f32[20,64,128]{2,1,0:T(8,128)S(1)}, s32[]{:T(128)}, bf16[8,20]{1,0:T(8,128)(2,1)S(1)}, ...), condition=%wide.region_7.8_spmd.clone, body=%wide.region_6.7_spmd.clone.sunk | while | flops 819224 | bytes 1638705 | solution.py:31
  113.4 8.9 %fusion.12 = f32[8,256,20,64]{1,3,2,0:T(8,128)S(1)} fusion(f32[8,20,256,64]{2,3,1,0:T(8,128)} %fusion.3, f32[8,256]{1,0:T(8,128)S(1)} %fusion.29, f32[20]{0:T(128)S(1)} %copy-done.4, f32[8,256,20]{1,2,0:T(8,128)S(1)} %copy.60, bf16[8,256,20,64]{1,0,3,2:T(8,128)(2,1)} %bitcast.84, bf16[8,256,128,1]{2,1,3,0:T(8,128)(2,1)S(1)} %bitcast.78, ...), kind=kOutput, calls=%fused_computation.23 | convolution fusion | flops 690749440 | bytes 32809680 | tf_op jit(solution)/shard_map/cin,chpn->cihp/dot_general | solution.py:87
  122.3 12.8 %copy.61 = f32[8,256,20,64]{1,0,3,2:T(8,128)} copy(f32[8,256,20,64]{1,3,2,0:T(8,128)S(1)} %fusion.12) | data formatting | bytes 20971520 | tf_op jit(solution)/shard_map/mul | solution.py:91
  135.1 9.4 %copy.68 = f32[160,8,8,256]{3,1,2,0:T(8,128)S(1)} copy(f32[160,8,8,256]{3,2,1,0:T(8,128)} %bitcast.81) | data formatting | bytes 20971520
  144.5 4.0 %copy-done.2 = f32[160,8,8,256]{3,1,2,0:T(8,128)} copy-done((f32[160,8,8,256]{3,1,2,0:T(8,128)}, f32[160,8,8,256]{3,1,2,0:T(8,128)S(1)}, u32[]{:S(2)}) %copy-start.2) | copy-done | bytes 10485784
  148.5 5.3 %multiply_reduce_fusion = f32[2048]{0:T(1024)S(1)} fusion(f32[2048,1280]{0,1:T(8,128)S(1)} %bitcast.79, bf16[2048,1280]{0,1:T(8,128)(2,1)} %copy.62), kind=kLoop, calls=%fused_computation.31 | loop fusion | flops 20969472 | bytes 15736832 | tf_op jit(solution)/shard_map/reduce_sum | solution.py:95
  153.8 12.0 %psum.7 = f32[2048]{0:T(1024)S(1)} all-reduce(f32[2048]{0:T(1024)S(1)} %multiply_reduce_fusion), channel_id=1, replica_groups=mesh['seq'=8,'head'=4] {'head'}, use_global_device_ids=true, to_apply=%region_9.10 | all-reduce | flops 2048 | bytes 16384 | tf_op jit(solution)/shard_map/psum | solution.py:95
  165.8 23.2 %convolution_convert_fusion = bf16[2048,2560]{1,0:T(8,128)(2,1)} fusion(bf16[1280,2560]{1,0:T(8,128)(2,1)} %param.23, f32[1280]{0:T(1024)S(1)} %copy-done.5, f32[2048]{0:T(1024)S(1)} %add_rsqrt_fusion, f32[2048,1280]{0,1:T(8,128)} %bitcast.80, bf16[2048,1280]{0,1:T(8,128)(2,1)} %copy.62), kind=kOutput, calls=%fused_computation.20 | convolution fusion | flops 13450608640 | bytes 32781312 | tf_op jit(solution)/shard_map/dot_general | solution.py:100
  189.0 174.4 %reduce-scatter.2.cloned.1.call-done = bf16[512,2560]{1,0:T(8,128)(2,1)} async-done(((bf16[2048,2560]{1,0:T(8,128)(2,1)}), bf16[512,2560]{1,0:T(8,128)(2,1)}) %reduce-scatter.2.cloned.1.call-update) | async-done | bytes 2621456 | tf_op jit(solution)/shard_map/reduce_scatter | solution.py:99
  (84 shorter events, 22.8 us)
Async XLA Ops:
  6.5 80.5 %copy-start = (bf16[2048,128]{1,0:T(8,128)(2,1)S(1)}, bf16[2048,128]{1,0:T(8,128)(2,1)}, u32[]{:S(2)}) copy-start(bf16[2048,128]{1,0:T(8,128)(2,1)} %param.18) | copy-start | bytes 1572868
  6.5 97.5 %all-gather.4.cloned.1.call-start = ((), (), s32[]{:S(2)}) async-start(), calls=%async_computation.2 | async-start | bytes 2949120 | tf_op jit(solution)/shard_map/all_gather | solution.py:14
  21.9 15.1 %copy-start.3 = (bf16[2048,128]{1,0:T(8,128)(2,1)S(1)}, bf16[2048,128]{1,0:T(8,128)(2,1)}, u32[]{:S(2)}) copy-start(bf16[2048,128]{1,0:T(8,128)(2,1)} %param.17) | copy-start | bytes 1572868
  43.4 18.1 %copy-start.6 = (u32[32]{0:T(128)S(1)}, u32[32]{0:T(128)}, u32[]{:S(2)}) copy-start(u32[32]{0:T(128)} %constant.74) | copy-start | bytes 388
  61.4 302.0 %reduce-scatter.2.cloned.1.call-start = ((), (), s32[]{:S(2)}) async-start(), calls=%async_computation.1 | async-start | bytes 13107200 | tf_op jit(solution)/shard_map/reduce_scatter | solution.py:99
  87.5 25.8 %copy-start.4 = (f32[20]{0:T(128)S(1)}, f32[20]{0:T(128)}, u32[]{:S(2)}) copy-start(f32[20]{0:T(128)} %param.21) | copy-start | bytes 244
  144.5 4.0 %copy-start.2 = (f32[160,8,8,256]{3,1,2,0:T(8,128)}, f32[160,8,8,256]{3,1,2,0:T(8,128)S(1)}, u32[]{:S(2)}) copy-start(f32[160,8,8,256]{3,1,2,0:T(8,128)S(1)} %copy.68) | copy-start | bytes 31457284
  144.5 21.3 %copy-start.5 = (f32[1280]{0:T(1024)S(1)}, f32[1280]{0:T(1024)}, u32[]{:S(2)}) copy-start(f32[1280]{0:T(1024)} %param.22) | copy-start | bytes 15364
  165.8 197.6 %copy-start.1 = (bf16[2048,128]{1,0:T(8,128)(2,1)S(1)}, bf16[2048,128]{1,0:T(8,128)(2,1)}, u32[]{:S(2)}) copy-start(bf16[2048,128]{1,0:T(8,128)(2,1)} %param.18) | copy-start | bytes 1572868
Sparse Core Ops, SparseCore 0:
  61.5 32.7 all-gather.3
  189.1 174.2 reduce-scatter.1
where the time goes:
time: 372 us; the launch traced here: 370 us
  waiting for transfers between devices  174 us (47%)
  matrix products  55.4 us (15%)
  local copies, waits for them, and re-layouts  51.7 us (14%)
  other arithmetic  45.1 us (12%)
  blocking collectives  27.5 us (7%)
  between operations  15.7 us (4%)
    reduce_scatter x1, waiting for transfers between devices, body(): lax.psum_scatter(jnp.dot(normed, readout_matrix, preferred_element_type=f...  174 us
    unnamed x22, local copies, waits for them, and re-layouts  37.6 us
    dot_general x1, matrix products, body(): jnp.dot(normed, readout_matrix, preferred_element_type=f32)  23.2 us
    dot_general x1, matrix products, body(): jnp.einsum('hcij,cjhp->cihp', mixing, heads_x, preferred_element_type=f32)  16.5 us
    unnamed x1, blocking collectives  15.6 us
    mul x1, local copies, waits for them, and re-layouts, body(): (inner + carried + skip_gain[None, None, :, None] * heads_x) * live.resha...  12.8 us
    psum x1, blocking collectives, body(): squares = lax.psum(jnp.sum(gated * gated, axis=1), 'head')  12 us
    another operation x2, other arithmetic  11.3 us
  transfers between devices with their start and end apart: 2, of which 1 were waited for; matrix products, arithmetic and copies ran while one was open for 7% of the time, Pallas kernels for 0%

commit v1 on v0

v1 whole, which is shorter than its diff:
```python
import functools
import math

import jax
import jax.numpy as jnp
from jax import lax
from jax.experimental import pallas as pl
from jax.experimental.pallas import tpu as pltpu
from jax.sharding import PartitionSpec as P

SPAN = 256
LOG2E = math.log2(math.e)
F32 = jnp.float32
BF16 = jnp.bfloat16
HIGH = lax.Precision.HIGHEST
MESH = pl.DeviceIdType.MESH
VMEM = pltpu.VMEM
LIMIT = 60 * 1024 * 1024


def contract(a, b, da, db, precision=None):
    return lax.dot_general(
        a, b, (((da,), (db,)), ((), ())), precision=precision, preferred_element_type=F32
    )


def expander(heads, width):
    size = width // heads
    col = lax.broadcasted_iota(jnp.int32, (heads, width), 1) // size
    row = lax.broadcasted_iota(jnp.int32, (heads, width), 0)
    return jnp.where(col == row, 1.0, 0.0).astype(F32)


def halves(a):
    hi = a.astype(BF16)
    return hi, (a - hi.astype(F32)).astype(BF16)


def state_kernel(
    valid_ref, x_ref, b_ref, st_ref, dr_ref, runT_ref, q_ref, before_ref, lead_ref, pack_ref, s_ref, l_ref
):
    heads, length = st_ref.shape
    width = x_ref.shape[1]
    blocks = length // SPAN
    i0 = lax.broadcasted_iota(jnp.int32, (SPAN, SPAN), 0)
    i1 = lax.broadcasted_iota(jnp.int32, (SPAN, SPAN), 1)
    tril = jnp.where(i0 >= i1, 1.0, 0.0).astype(F32)
    spread = expander(heads, width)
    spread16 = spread.astype(BF16)
    s_ref[...] = jnp.zeros_like(s_ref)
    l_ref[...] = jnp.ones_like(l_ref)

    def step(c, carry):
        at = pl.ds(pl.multiple_of(c * SPAN, SPAN), SPAN)
        slot = c * SPAN + lax.broadcasted_iota(jnp.int32, (heads, SPAN), 1)
        live = slot < valid_ref[0]
        ld = jnp.where(live, dr_ref[:, at] * (-LOG2E), 0.0)
        run = contract(ld, tril, 1, 1, HIGH)
        runT = contract(tril, ld, 1, 1, HIGH)
        q = jnp.where(live, run - jnp.log2(st_ref[:, at]), 1e30)
        runT_ref[at, :] = runT
        q_ref[:, at] = q
        tail = jnp.exp2(run[:, SPAN - 1 :] - q)
        hi, lo = halves(tail)
        texp = contract(hi, spread16, 0, 0) + contract(lo, spread16, 0, 0)
        weighted = (x_ref[at, :].astype(F32) * texp).astype(BF16)
        fresh = contract(b_ref[at, :], weighted, 0, 0)
        dec = contract(jnp.exp2(runT[SPAN - 8 :, :]), spread, 1, 0, HIGH)[7:8, :]
        before_ref[c] = s_ref[...]
        lead_ref[c] = l_ref[...]
        s_ref[...] = dec * s_ref[...] + fresh
        l_ref[...] = l_ref[...] * dec
        return carry

    lax.fori_loop(0, blocks, step, 0)
    state = s_ref.shape[0]
    pack_ref[0:state, :] = s_ref[...].astype(BF16)
    total = jnp.broadcast_to(l_ref[0:1, :], (16, width))
    hi, mid = halves(total)
    low = (total - hi.astype(F32) - mid.astype(F32)).astype(BF16)
    row = lax.broadcasted_iota(jnp.int32, (16, width), 0)
    parts = jnp.where(row == 0, hi.astype(F32), jnp.where(row == 1, mid.astype(F32), low.astype(F32)))
    pack_ref[state:, :] = jnp.where(row < 3, parts, 0.0).astype(BF16)


def mix_kernel(
    ranks,
    x_ref,
    g_ref,
    b_ref,
    c_ref,
    runT_ref,
    q_ref,
    before_ref,
    lead_ref,
    all_ref,
    skip_ref,
    gain_ref,
    got_ref,
    ss_ref,
    out_buf,
    ss_buf,
    inc_ref,
    send_sem,
    recv_sem,
    ssend_sem,
    srecv_sem,
):
    heads, length = q_ref.shape
    width = x_ref.shape[1]
    blocks = length // SPAN
    each = blocks // ranks
    state = before_ref.shape[1]
    shards = all_ref.shape[0]
    me = lax.axis_index("head")
    place = lax.axis_index("seq")

    barrier = pltpu.get_barrier_semaphore()
    for k in range(1, ranks):
        pl.semaphore_signal(
            barrier, inc=1, device_id={"head": lax.rem(me + k, ranks)}, device_id_type=MESH
        )
    pl.semaphore_wait(barrier, ranks - 1)

    inc_ref[...] = jnp.zeros_like(inc_ref)

    def lap(k, carry):
        tail = all_ref[k, state:, :].astype(F32)
        decay = tail[0:1, :] + tail[1:2, :] + tail[2:3, :]
        new = decay * inc_ref[...] + all_ref[k, 0:state, :].astype(F32)
        inc_ref[...] = jnp.where(k < place, new, inc_ref[...])
        return carry

    lax.fori_loop(0, shards, lap, 0)

    spread16 = expander(heads, width).astype(BF16)
    i0 = lax.broadcasted_iota(jnp.int32, (SPAN, SPAN), 0)
    i1 = lax.broadcasted_iota(jnp.int32, (SPAN, SPAN), 1)
    lower = i0 >= i1
    left = lax.broadcasted_iota(jnp.int32, (SPAN, 128), 1) < (width // heads)
    ones = jnp.ones((8, 128), F32)

    def copies(dest, j, slot):
        c = dest * each + j
        at = pl.ds(pl.multiple_of(c * SPAN, SPAN), SPAN)
        big = pltpu.make_async_remote_copy(
            src_ref=out_buf.at[at, :],
            dst_ref=got_ref.at[slot, pl.ds(j * SPAN, SPAN), :],
            send_sem=send_sem.at[slot, j],
            recv_sem=recv_sem.at[slot, j],
            device_id={"head": dest},
            device_id_type=MESH,
        )
        small = pltpu.make_async_remote_copy(
            src_ref=ss_buf.at[c],
            dst_ref=ss_ref.at[slot, j],
            send_sem=ssend_sem.at[slot, j],
            recv_sem=srecv_sem.at[slot, j],
            device_id={"head": dest},
            device_id_type=MESH,
        )
        return big, small

    def local(j):
        c = me * each + j
        at = pl.ds(pl.multiple_of(c * SPAN, SPAN), SPAN)
        big = pltpu.make_async_copy(
            out_buf.at[at, :], got_ref.at[0, pl.ds(j * SPAN, SPAN), :], send_sem.at[0, j]
        )
        small = pltpu.make_async_copy(ss_buf.at[c], ss_ref.at[0, j], ssend_sem.at[0, j])
        return big, small

    def span(c):
        at = pl.ds(pl.multiple_of(c * SPAN, SPAN), SPAN)
        cb = c_ref[at, :]
        gram = jnp.where(lower, contract(cb, b_ref[at, :], 1, 1), 0.0)
        held = (before_ref[c] + lead_ref[c, 0:1, :] * inc_ref[...]).astype(BF16)
        runT = runT_ref[at, :]
        q = q_ref[:, at]
        hi, lo = halves(jnp.exp2(runT))
        acc = jnp.zeros((SPAN, 128), F32)
        for p in range(width // 128):
            cols = slice(p * 128, p * 128 + 128)
            xp = x_ref[at, cols]
            grow = contract(hi, spread16[:, cols], 1, 0) + contract(lo, spread16[:, cols], 1, 0)
            carried = contract(cb, held[:, cols], 1, 0) * grow
            sides = []
            for h in (2 * p, 2 * p + 1):
                m = (
                    gram * jnp.exp2(jnp.minimum(runT[:, h : h + 1] - q[h : h + 1, :], 0.0))
                ).astype(BF16)
                sides.append(jnp.dot(m, xp, preferred_element_type=F32))
            inner = jnp.where(left, sides[0], sides[1])
            z = g_ref[at, cols].astype(F32)
            gated = (inner + carried + skip_ref[:, cols] * xp.astype(F32)) * (
                z * (0.5 * jnp.tanh(0.5 * z) + 0.5)
            )
            acc = acc + gated * gated
            out_buf[at, cols] = (gated * gain_ref[:, cols]).astype(BF16)
        ss_buf[c] = contract(ones, acc, 1, 1, HIGH)

    if ranks == 4:
        order = [ranks - 1 - me, lax.rem(me + 2, ranks), me + 1 - 2 * lax.rem(me, 2)]
    else:
        order = [lax.rem(me + k, ranks) for k in range(1, ranks)]
    for index, dest in enumerate(order):
        slot = lax.rem(me - dest + ranks, ranks)

        def one(j, carry, dest=dest, slot=slot):
            span(dest * each + j)
            for copy in copies(dest, j, slot):
                copy.start()
            return carry

        lax.fori_loop(0, each, one, 0)

    def mine(j, carry):
        span(me * each + j)
        for copy in local(j):
            copy.start()
        return carry

    lax.fori_loop(0, each, mine, 0)
    for j in range(each):
        for copy in local(j):
            copy.wait()
        for dest in order:
            slot = lax.rem(me - dest + ranks, ranks)
            for copy in copies(dest, j, slot):
                copy.wait_send()
        for slot in range(1, ranks):
            for copy in copies(lax.rem(me + slot, ranks), j, slot):
                copy.wait_recv()


def body(
    ranks,
    shards,
    values,
    gates,
    b_proj,
    c_proj,
    step_size,
    decay_rate,
    skip_gain,
    norm_gain,
    readout,
    span_counts,
    remaining_count,
):
    length, width = values.shape
    heads = step_size.shape[0]
    state = b_proj.shape[1]
    blocks = length // SPAN
    me = lax.axis_index("head")
    place = lax.axis_index("seq")
    valid = (span_counts - 1) * SPAN + remaining_count
    sds = jax.ShapeDtypeStruct
    whole = pl.BlockSpec(memory_space=VMEM)

    rows = readout.shape[0] // shards
    own = lax.dynamic_slice_in_dim(readout, place * rows, rows, 0)
    moved = [
        lax.ppermute(own, "head", [((i + r) % ranks, i) for i in range(ranks)])
        for r in range(1, ranks)
    ]

    runT, q, before, lead, pack = pl.pallas_call(
        state_kernel,
        out_shape=(
            sds((length, heads), F32),
            sds((heads, length), F32),
            sds((blocks, state, width), F32),
            sds((blocks, 8, width), F32),
            sds((state + 16, width), BF16),
        ),
        in_specs=[pl.BlockSpec(memory_space=pltpu.SMEM)] + [whole] * 4,
        out_specs=(whole,) * 5,
        scratch_shapes=[VMEM((state, width), F32), VMEM((8, width), F32)],
        compiler_params=pltpu.CompilerParams(vmem_limit_bytes=LIMIT),
        cost_estimate=pl.CostEstimate(flops=10**10, bytes_accessed=12 * 10**6, transcendentals=0),
        name="span_states",
    )(valid, values, b_proj, step_size, decay_rate)

    everyone = lax.all_gather(pack, "seq")
    moved, everyone = lax.optimization_barrier((moved, everyone))
    mats = [readout] + [lax.all_gather(m, "seq", tiled=True) for m in moved]

    share = length // ranks
    each = blocks // ranks
    got, ss = pl.pallas_call(
        functools.partial(mix_kernel, ranks),
        out_shape=(sds((ranks, share, width), BF16), sds((ranks, each, 8, SPAN), F32)),
        in_specs=[whole] * 11,
        out_specs=(pl.BlockSpec(memory_space=pl.ANY), pl.BlockSpec(memory_space=pl.ANY)),
        scratch_shapes=[
            VMEM((length, width), BF16),
            VMEM((blocks, 8, SPAN), F32),
            VMEM((state, width), F32),
            pltpu.SemaphoreType.DMA((ranks, each)),
            pltpu.SemaphoreType.DMA((ranks, each)),
            pltpu.SemaphoreType.DMA((ranks, each)),
            pltpu.SemaphoreType.DMA((ranks, each)),
        ],
        compiler_params=pltpu.CompilerParams(
            vmem_limit_bytes=LIMIT, collective_id=0, has_side_effects=True
        ),
        cost_estimate=pl.CostEstimate(flops=10**11, bytes_accessed=20 * 10**6, transcendentals=0),
        name="mix_and_send",
    )(
        values,
        gates,
        b_proj,
        c_proj,
        runT,
        q,
        before,
        lead,
        everyone,
        jnp.repeat(skip_gain, width // heads)[None, :],
        norm_gain[None, :],
    )

    total = jnp.sum(ss[:, :, 0, :], axis=0).reshape(share) / (width * ranks)
    live = me * share + jnp.arange(share, dtype=jnp.int32) < valid[0]
    scale = jnp.where(live, lax.rsqrt(total + 1e-05), 0.0)
    out = sum(jnp.dot(got[r], mats[r], preferred_element_type=F32) for r in range(ranks))
    return (out * scale[:, None]).astype(BF16)


def solution(mesh):
    return jax.shard_map(
        functools.partial(body, mesh.shape["head"], mesh.shape["seq"]),
        mesh=mesh,
        in_specs=(
            P("seq", "head"),
            P("seq", "head"),
            P("seq", None),
            P("seq", None),
            P("head", "seq"),
            P("head", "seq"),
            P("head"),
            P("head"),
            P("head", None),
            P("seq"),
            P("seq"),
        ),
        out_specs=P(("seq", "head"), None),
        check_vma=False,
    )
```

time: 372 us -> 281 us (0.76)
  Pallas kernels: 0 us -> 162 us
  waiting for transfers between devices: 174 us -> 52.2 us
  local copies, waits for them, and re-layouts: 51.7 us -> 3.62 us
  other arithmetic: 45.1 us -> 0.88 us
  blocking collectives: 27.5 us -> 0 us
  matrix products: 55.4 us -> 40.5 us
  starting transfers between devices: 0.04 us -> 7.16 us
    reduce_scatter x1 -> x0, waiting for transfers between devices: 174 us -> none  [body(): lax.psum_scatter(jnp.dot(normed, readout_matrix, preferred_element_type=f...]
    pallas_call x0 -> x2, Pallas kernels: none -> 162 us  [the longest x1 145 us: body(): pl.pallas_call(functools.partial(mix_kernel, ranks), out_shape=(sds((rank...]
    ppermute x0 -> x3, waiting for transfers between devices: none -> 51.5 us  [body(): lax.ppermute(own, 'head', [((i + r) % ranks, i) for i in range(ranks)])]
    unnamed x22 -> x11, local copies, waits for them, and re-layouts: 37.6 us -> 1.08 us
    unnamed x1 -> x0, blocking collectives: 15.6 us -> none
    dot_general x5 -> x4, matrix products: 55.4 us -> 40.5 us  [body(): jnp.dot(got[r], mats[r], preferred_element_type=F32)]
    mul x2 -> x0, local copies, waits for them, and re-layouts: 12.9 us -> none  [the longest x1 12.8 us: body(): (inner + carried + skip_gain[None, None, :, None] * heads_x) * live.resha...]
    psum x1 -> x0, blocking collectives: 12 us -> none  [body(): squares = lax.psum(jnp.sum(gated * gated, axis=1), 'head')]
  transfers between devices with their start and end apart: 2 -> 7, of which waited for: 1 -> 2; matrix products, arithmetic and copies ran while one was open for 7% -> 11% of each run, Pallas kernels for 0% -> 52%
where the time goes in v1:
time: 281 us
  Pallas kernels  162 us (58%)
  waiting for transfers between devices  52.2 us (19%)
  matrix products  40.5 us (14%)
  between operations  14.5 us (5%)
  starting transfers between devices  7.16 us (3%)
  local copies, waits for them, and re-layouts  3.62 us (1%)
    pallas_call x1, Pallas kernels, body(): pl.pallas_call(functools.partial(mix_kernel, ranks), out_shape=(sds((rank...  145 us
    ppermute x3, waiting for transfers between devices, body(): lax.ppermute(own, 'head', [((i + r) % ranks, i) for i in range(ranks)])  51.5 us
    dot_general x4, matrix products, body(): jnp.dot(got[r], mats[r], preferred_element_type=F32)  40.5 us
    pallas_call x1, Pallas kernels, body(): pl.pallas_call(state_kernel, out_shape=(sds((length, heads), F32), sds((h...  16.8 us
    ppermute x3, starting transfers between devices, body(): lax.ppermute(own, 'head', [((i + r) % ranks, i) for i in range(ranks)])  7.04 us
  transfers between devices with their start and end apart: 7, of which 2 were waited for; matrix products, arithmetic and copies ran while one was open for 11% of the time, Pallas kernels for 52%

profile of v1, /device:TPU:0, one launch (start us, length us, event | category | flops | bytes accessed | tf_op | source)
XLA Modules:
  0.0 280.9 jit_solution(17959811888389066682)
XLA Ops:
  7.9 16.8 %span_states.1 = (f32[2048,20]{1,0:T(8,128)}, f32[20,2048]{1,0:T(8,128)}, f32[8,128,1280]{2,1,0:T(8,128)}, f32[8,8,1280]{2,1,0:T(8,128)}, bf16[144,1280]{1,0:T(8,128)(2,1)}) custom-call(s32[1]{0:T(128)} %add.37.valid_ref, bf16[2048,1280]{1,0:T(8,128)(2,1)} %x_ref.3, bf16[2048,128]{1,0:T(8,128)(2,1)} %b_ref.3, f32[20,2048]{1,0:T(8,128)} %st_ref.1, ...), custom_call_target="tpu_custom_call" | custom-call | flops 10000000000 | bytes 12000000 | tf_op jit(solution)/shard_map/span_states/pallas_call | solution.py:268
  24.7 0.0 all-gather.12.cloned.1.call-update
  24.7 0.0 all-gather.6.cloned.1.call-start
  24.7 1.2 constant_dynamic-slice_fusion
  25.9 3.1 %collective-permute-start.2 = (bf16[160,2560]{1,0:T(8,128)(2,1)S(1)}, bf16[160,2560]{1,0:T(8,128)(2,1)S(1)}, u32[]{:S(2)}, u32[]{:S(2)}) collective-permute-start(bf16[160,2560]{1,0:T(8,128)(2,1)S(1)} %constant_dynamic-slice_fusion), channel_id=1, source_target_pairs={{3,0},{0,1},{1,2},{2,3},{7,4},{4,5},{5,6},{6,7},{11,8},{8,9},{9,10... | collective-permute-start | bytes 2457608 | tf_op jit(solution)/shard_map/ppermute | solution.py:264
  29.0 2.6 collective-permute-start.1
  31.6 1.4 collective-permute-start
  33.0 17.3 %collective-permute-done.2 = bf16[160,2560]{1,0:T(8,128)(2,1)S(1)} collective-permute-done((bf16[160,2560]{1,0:T(8,128)(2,1)S(1)}, bf16[160,2560]{1,0:T(8,128)(2,1)S(1)}, u32[]{:S(2)}, u32[]{:S(2)}) %collective-permute-start.2) | collective-permute-done | bytes 819232 | tf_op jit(solution)/shard_map/ppermute | solution.py:264
  50.3 34.3 %collective-permute-done.1 = bf16[160,2560]{1,0:T(8,128)(2,1)S(1)} collective-permute-done((bf16[160,2560]{1,0:T(8,128)(2,1)S(1)}, bf16[160,2560]{1,0:T(8,128)(2,1)S(1)}, u32[]{:S(2)}, u32[]{:S(2)}) %collective-permute-start.1) | collective-permute-done | bytes 819232 | tf_op jit(solution)/shard_map/ppermute | solution.py:264
  84.6 0.9 copy-done.2
  85.5 0.0 all-gather.8.cloned.1.call-start
  85.6 0.1 copy-done.1
  85.7 0.6 all-gather.8.cloned.1.call-update
  86.2 0.0 all-gather.10.cloned.1.call-start
  86.3 0.6 broadcast_in_dim.12.gain_ref
  86.9 0.1 broadcast_in_dim.11
  87.0 0.7 broadcast_in_dim_reshape.3.skip_ref
  87.7 0.0 all-gather.10.cloned.1.call-update
  87.7 145.2 %mix_and_send.1 = (bf16[4,512,1280]{2,1,0:T(8,128)(2,1)}, f32[4,2,8,256]{3,2,1,0:T(8,128)}) custom-call(bf16[2048,1280]{1,0:T(8,128)(2,1)} %x_ref.3, bf16[2048,1280]{1,0:T(8,128)(2,1)} %g_ref.1, bf16[2048,128]{1,0:T(8,128)(2,1)} %b_ref.3, bf16[2048,128]{1,0:T(8,128)(2,1)} %c_ref.1, f32[2048,20]{1,0:T(8,128)} %get-tuple-element.16.runT_ref, ...), custom_call_target="tpu_custom_call" | custom-call | flops 99999997952 | bytes 20000000 | tf_op jit(solution)/shard_map/mix_and_send/pallas_call | solution.py:291
  232.9 0.9 slice_reduce_fusion
  233.8 9.3 %fusion.5 = f32[512,2560]{1,0:T(8,128)} fusion(bf16[1280,2560]{1,0:T(8,128)(2,1)} %param.19, bf16[4,512,1280]{2,1,0:T(8,128)(2,1)} %get-tuple-element.22), kind=kOutput, calls=%fused_computation.6 | convolution fusion | flops 3355443200 | bytes 13107200 | tf_op jit(solution)/shard_map/dot_general | solution.py:327
  243.1 9.2 %fusion.3 = f32[512,2560]{1,0:T(8,128)} fusion(bf16[1280,2560]{1,0:T(8,128)(2,1)} %all-gather.6.cloned.1.call-done, bf16[4,512,1280]{2,1,0:T(8,128)(2,1)} %get-tuple-element.22), kind=kOutput, calls=%fused_computation.4 | convolution fusion | flops 3355443200 | bytes 13107200 | tf_op jit(solution)/shard_map/dot_general | solution.py:327
  252.3 9.1 %fusion.1 = f32[512,2560]{1,0:T(8,128)} fusion(bf16[1280,2560]{1,0:T(8,128)(2,1)} %all-gather.8.cloned.1.call-done, bf16[4,512,1280]{2,1,0:T(8,128)(2,1)} %get-tuple-element.22), kind=kOutput, calls=%fused_computation.2 | convolution fusion | flops 3355443200 | bytes 13107200 | tf_op jit(solution)/shard_map/dot_general | solution.py:327
  261.4 12.9 %multiply_convert_fusion = bf16[512,2560]{1,0:T(8,128)(2,1)} fusion(f32[512,2560]{1,0:T(8,128)} %fusion.1, f32[512,2560]{1,0:T(8,128)} %fusion.5, f32[512,2560]{1,0:T(8,128)} %fusion.3, bf16[1280,2560]{1,0:T(8,128)(2,1)} %all-gather.10.cloned.1.call-done, f32[512]{0:T(512)S(1)} %fusion.11, bf16[4,512,1280]{2,1,0:T(8,128)(2,1)} %get-tuple-element.22), kind=kOutput, calls=%fused_computation | convolution fusion | flops 3361996800 | bytes 26216448 | tf_op jit(solution)/shard_map/dot_general | solution.py:327
  (18 shorter events, 0.1 us)
Async XLA Ops:
  6.5 78.0 %all-gather.12.cloned.1.call-start = ((), (), s32[]{:S(2)}) async-start(), calls=%async_computation.3 | async-start | bytes 3317760 | tf_op jit(solution)/shard_map/all_gather | solution.py:285
  7.8 78.5 %copy-start.3 = (f32[1280]{0:T(1024)S(1)}, f32[1280]{0:T(1024)}, u32[]{:S(2)}) copy-start(f32[1280]{0:T(1024)} %param.18) | copy-start | bytes 15364
  7.8 79.0 %copy-start.4 = (f32[20]{0:T(128)S(1)}, f32[20]{0:T(128)}, u32[]{:S(2)}) copy-start(f32[20]{0:T(128)} %param.17) | copy-start | bytes 244
  24.7 218.4 %all-gather.6.cloned.1.call-start = ((), (), s32[]{:S(2)}) async-start(), calls=%async_computation | async-start | bytes 7372800 | tf_op jit(solution)/shard_map/all_gather | solution.py:287
  25.9 24.3 %collective-permute-start.2 = (bf16[160,2560]{1,0:T(8,128)(2,1)S(1)}, bf16[160,2560]{1,0:T(8,128)(2,1)S(1)}, u32[]{:S(2)}, u32[]{:S(2)}) collective-permute-start(bf16[160,2560]{1,0:T(8,128)(2,1)S(1)} %constant_dynamic-slice_fusion), channel_id=1, source_target_pairs={{3,0},{0,1},{1,2},{2,3},{7,4},{4,5},{5,6},{6,7},{11,8},{8,9},{9,10... | collective-permute-start | bytes 2457608 | tf_op jit(solution)/shard_map/ppermute | solution.py:264
  29.0 55.5 %collective-permute-start.1 = (bf16[160,2560]{1,0:T(8,128)(2,1)S(1)}, bf16[160,2560]{1,0:T(8,128)(2,1)S(1)}, u32[]{:S(2)}, u32[]{:S(2)}) collective-permute-start(bf16[160,2560]{1,0:T(8,128)(2,1)S(1)} %constant_dynamic-slice_fusion), channel_id=1, source_target_pairs={{2,0},{3,1},{0,2},{1,3},{6,4},{7,5},{4,6},{5,7},{10,8},{11,9},{8,1... | collective-permute-start | bytes 2457608 | tf_op jit(solution)/shard_map/ppermute | solution.py:264
  31.6 52.9 %collective-permute-start = (bf16[160,2560]{1,0:T(8,128)(2,1)S(1)}, bf16[160,2560]{1,0:T(8,128)(2,1)S(1)}, u32[]{:S(2)}, u32[]{:S(2)}) collective-permute-start(bf16[160,2560]{1,0:T(8,128)(2,1)S(1)} %constant_dynamic-slice_fusion), channel_id=1, source_target_pairs={{1,0},{2,1},{3,2},{0,3},{5,4},{6,5},{7,6},{4,7},{9,8},{10,9},{11,1... | collective-permute-start | bytes 2457608 | tf_op jit(solution)/shard_map/ppermute | solution.py:264
  50.3 37.4 %copy-start = (bf16[160,2560]{1,0:T(8,128)(2,1)}, bf16[160,2560]{1,0:T(8,128)(2,1)S(1)}, u32[]{:S(2)}) copy-start(bf16[160,2560]{1,0:T(8,128)(2,1)S(1)} %collective-permute-done.2) | copy-start | bytes 2457604
  84.5 1.2 copy-start.1
  84.5 1.0 copy-start.2
  85.5 166.8 %all-gather.8.cloned.1.call-start = ((), (), s32[]{:S(2)}) async-start(), calls=%async_computation.1 | async-start | bytes 7372800 | tf_op jit(solution)/shard_map/all_gather | solution.py:287
  86.2 175.2 %all-gather.10.cloned.1.call-start = ((), (), s32[]{:S(2)}) async-start(), calls=%async_computation.2 | async-start | bytes 7372800 | tf_op jit(solution)/shard_map/all_gather | solution.py:287
Sparse Core Ops, SparseCore 0:
  24.8 34.0 all-gather.11
  85.6 63.2 all-gather.5
  150.8 46.4 all-gather.7
  199.1 46.4 all-gather.9

commit v2 on v1

--- a/solution.py
+++ b/solution.py
@@ -7,6 +7,7 @@
 from jax.experimental import pallas as pl
 from jax.experimental.pallas import tpu as pltpu
 from jax.sharding import PartitionSpec as P
+
 
 SPAN = 256
 LOG2E = math.log2(math.e)
@@ -203,7 +204,7 @@
         order = [ranks - 1 - me, lax.rem(me + 2, ranks), me + 1 - 2 * lax.rem(me, 2)]
     else:
         order = [lax.rem(me + k, ranks) for k in range(1, ranks)]
-    for index, dest in enumerate(order):
+    for dest in order:
         slot = lax.rem(me - dest + ranks, ranks)
 
         def one(j, carry, dest=dest, slot=slot):
@@ -231,6 +232,14 @@
         for slot in range(1, ranks):
             for copy in copies(lax.rem(me + slot, ranks), j, slot):
                 copy.wait_recv()
+
+
+def readout_kernel(got_ref, scale_ref, *refs):
+    total = None
+    for r, mat in enumerate(refs[:-1]):
+        part = jnp.dot(got_ref[r], mat[...], preferred_element_type=F32)
+        total = part if total is None else total + part
+    refs[-1][...] = (total * scale_ref[...]).astype(BF16)
 
 
 def body(
@@ -265,7 +274,7 @@
         for r in range(1, ranks)
     ]
 
-    runT, q, before, lead, pack = pl.pallas_call(
+    spans = pl.pallas_call(
         state_kernel,
         out_shape=(
             sds((length, heads), F32),
@@ -280,7 +289,8 @@
         compiler_params=pltpu.CompilerParams(vmem_limit_bytes=LIMIT),
         cost_estimate=pl.CostEstimate(flops=10**10, bytes_accessed=12 * 10**6, transcendentals=0),
         name="span_states",
-    )(valid, values, b_proj, step_size, decay_rate)
+    )
+    runT, q, before, lead, pack = spans(valid, values, b_proj, step_size, decay_rate)
 
     everyone = lax.all_gather(pack, "seq")
     moved, everyone = lax.optimization_barrier((moved, everyone))
@@ -324,8 +334,24 @@
     total = jnp.sum(ss[:, :, 0, :], axis=0).reshape(share) / (width * ranks)
     live = me * share + jnp.arange(share, dtype=jnp.int32) < valid[0]
     scale = jnp.where(live, lax.rsqrt(total + 1e-05), 0.0)
-    out = sum(jnp.dot(got[r], mats[r], preferred_element_type=F32) for r in range(ranks))
-    return (out * scale[:, None]).astype(BF16)
+    depth = readout.shape[1]
+    tile = 256
+    return pl.pallas_call(
+        readout_kernel,
+        grid=(depth // tile,),
+        out_shape=sds((share, depth), BF16),
+        in_specs=[
+            pl.BlockSpec((ranks, share, width), lambda n: (0, 0, 0)),
+            pl.BlockSpec((share, 1), lambda n: (0, 0)),
+        ]
+        + [pl.BlockSpec((width, tile), lambda n: (0, n))] * ranks,
+        out_specs=pl.BlockSpec((share, tile), lambda n: (0, n)),
+        compiler_params=pltpu.CompilerParams(vmem_limit_bytes=LIMIT),
+        cost_estimate=pl.CostEstimate(
+            flops=2 * share * width * ranks * depth, bytes_accessed=35 * 10**6, transcendentals=0
+        ),
+        name="readout",
+    )(got, scale[:, None], *mats)
 
 
 def solution(mesh):

time: 281 us -> 274 us (0.975)
  matrix products: 40.5 us -> 0 us
  Pallas kernels: 162 us -> 183 us
  waiting for transfers between devices: 52.2 us -> 62.8 us
    dot_general x4 -> x0, matrix products: 40.5 us -> none  [body(): jnp.dot(got[r], mats[r], preferred_element_type=F32)]
    pallas_call x1 -> x2, Pallas kernels: 16.8 us -> 37.6 us  [the longest x1 20.9 us: body(): pl.pallas_call(readout_kernel, grid=(depth // tile,), out_shape=sds((shar...]
    all_gather x3, waiting for transfers between devices: 0.01 us -> 10.2 us  [body(): mats = [readout] + [lax.all_gather(m, 'seq', tiled=True) for m in moved]]
  transfers between devices with their start and end apart: 7 -> 7, of which waited for: 2 -> 3; matrix products, arithmetic and copies ran while one was open for 11% -> 2% of each run, Pallas kernels for 52% -> 53%
where the time goes in v2:
time: 274 us; the launch traced here: 273 us
  Pallas kernels  183 us (67%)
  waiting for transfers between devices  62.8 us (23%)
  between operations  14.5 us (5%)
  starting transfers between devices  7.16 us (3%)
  local copies, waits for them, and re-layouts  3.8 us (1%)
    pallas_call x1, Pallas kernels, body(): pl.pallas_call(functools.partial(mix_kernel, ranks), out_shape=(sds((rank...  145 us
    ppermute x3, waiting for transfers between devices, body(): lax.ppermute(own, 'head', [((i + r) % ranks, i) for i in range(ranks)])  51.6 us
    pallas_call x1, Pallas kernels, body(): pl.pallas_call(readout_kernel, grid=(depth // tile,), out_shape=sds((shar...  20.9 us
    pallas_call x1, Pallas kernels, body(): spans(valid, values, b_proj, step_size, decay_rate)  16.8 us
    all_gather x3, waiting for transfers between devices, body(): mats = [readout] + [lax.all_gather(m, 'seq', tiled=True) for m in moved]  10.2 us
    ppermute x3, starting transfers between devices, body(): lax.ppermute(own, 'head', [((i + r) % ranks, i) for i in range(ranks)])  7.04 us
  transfers between devices with their start and end apart: 7, of which 3 were waited for; matrix products, arithmetic and copies ran while one was open for 2% of the time, Pallas kernels for 53%

profile of v2, /device:TPU:0, one launch (start us, length us, event | category | flops | bytes accessed | tf_op | source)
XLA Modules:
  0.0 273.0 jit_solution(14749017312173155106)
XLA Ops:
  7.9 16.8 %span_states.1 = (f32[2048,20]{1,0:T(8,128)}, f32[20,2048]{1,0:T(8,128)}, f32[8,128,1280]{2,1,0:T(8,128)}, f32[8,8,1280]{2,1,0:T(8,128)}, bf16[144,1280]{1,0:T(8,128)(2,1)}) custom-call(s32[1]{0:T(128)} %add.34.valid_ref, bf16[2048,1280]{1,0:T(8,128)(2,1)} %x_ref.3, bf16[2048,128]{1,0:T(8,128)(2,1)} %b_ref.3, f32[20,2048]{1,0:T(8,128)} %st_ref.1, ...), custom_call_target="tpu_custom_call" | custom-call | flops 10000000000 | bytes 12000000 | tf_op jit(solution)/shard_map/span_states/pallas_call | solution.py:293
  24.6 0.0 all-gather.12.cloned.1.call-update
  24.6 0.0 all-gather.6.cloned.1.call-start
  24.7 1.2 constant_dynamic-slice_fusion
  25.9 3.1 %collective-permute-start.2 = (bf16[160,2560]{1,0:T(8,128)(2,1)S(1)}, bf16[160,2560]{1,0:T(8,128)(2,1)S(1)}, u32[]{:S(2)}, u32[]{:S(2)}) collective-permute-start(bf16[160,2560]{1,0:T(8,128)(2,1)S(1)} %constant_dynamic-slice_fusion), channel_id=1, source_target_pairs={{3,0},{0,1},{1,2},{2,3},{7,4},{4,5},{5,6},{6,7},{11,8},{8,9},{9,10... | collective-permute-start | bytes 2457608 | tf_op jit(solution)/shard_map/ppermute | solution.py:273
  29.0 2.6 collective-permute-start.1
  31.6 1.3 collective-permute-start
  32.9 17.3 %collective-permute-done.2 = bf16[160,2560]{1,0:T(8,128)(2,1)S(1)} collective-permute-done((bf16[160,2560]{1,0:T(8,128)(2,1)S(1)}, bf16[160,2560]{1,0:T(8,128)(2,1)S(1)}, u32[]{:S(2)}, u32[]{:S(2)}) %collective-permute-start.2) | collective-permute-done | bytes 819232 | tf_op jit(solution)/shard_map/ppermute | solution.py:273
  50.3 34.3 %collective-permute-done.1 = bf16[160,2560]{1,0:T(8,128)(2,1)S(1)} collective-permute-done((bf16[160,2560]{1,0:T(8,128)(2,1)S(1)}, bf16[160,2560]{1,0:T(8,128)(2,1)S(1)}, u32[]{:S(2)}, u32[]{:S(2)}) %collective-permute-start.1) | collective-permute-done | bytes 819232 | tf_op jit(solution)/shard_map/ppermute | solution.py:273
  84.5 0.9 copy-done.2
  85.5 0.0 all-gather.8.cloned.1.call-start
  85.5 0.2 copy-done.1
  85.7 0.5 all-gather.8.cloned.1.call-update
  86.2 0.0 all-gather.10.cloned.1.call-start
  86.3 0.5 all-gather.10.cloned.1.call-update
  86.8 0.6 broadcast_in_dim.12.gain_ref
  87.4 0.1 broadcast_in_dim.11
  87.5 0.7 broadcast_in_dim_reshape.3.skip_ref
  88.2 145.4 %mix_and_send.1 = (bf16[4,512,1280]{2,1,0:T(8,128)(2,1)}, f32[4,2,8,256]{3,2,1,0:T(8,128)}) custom-call(bf16[2048,1280]{1,0:T(8,128)(2,1)} %x_ref.3, bf16[2048,1280]{1,0:T(8,128)(2,1)} %g_ref.1, bf16[2048,128]{1,0:T(8,128)(2,1)} %b_ref.3, bf16[2048,128]{1,0:T(8,128)(2,1)} %c_ref.1, f32[2048,20]{1,0:T(8,128)} %get-tuple-element.16.runT_ref, ...), custom_call_target="tpu_custom_call" | custom-call | flops 99999997952 | bytes 20000000 | tf_op jit(solution)/shard_map/mix_and_send/pallas_call | solution.py:301
  233.6 0.9 slice_reduce_fusion
  234.5 0.1 copy.14
  234.6 0.8 bitcast_select_fusion.scale_ref
  235.4 10.2 %all-gather.10.cloned.1.call-done.refs_3_ = bf16[1280,2560]{1,0:T(8,128)(2,1)} async-done(((bf16[160,2560]{1,0:T(8,128)(2,1)}), bf16[1280,2560]{1,0:T(8,128)(2,1)}) %all-gather.10.cloned.1.call-update) | async-done | bytes 6553616 | tf_op jit(solution)/shard_map/all_gather | solution.py:297
  245.6 20.9 %readout.1 = bf16[512,2560]{1,0:T(8,128)(2,1)} custom-call(bf16[4,512,1280]{2,1,0:T(8,128)(2,1)} %get-tuple-element.22.got_ref, f32[512,1]{1,0:T(8,128)} %bitcast_select_fusion.scale_ref, bf16[1280,2560]{1,0:T(8,128)(2,1)} %refs_0_.1, bf16[1280,2560]{1,0:T(8,128)(2,1)} %all-gather.6.cloned.1.call-done.refs_1_, ...), custom_call_target="tpu_custom_call" | custom-call | flops 13421772800 | bytes 35000000 | tf_op jit(solution)/shard_map/readout/pallas_call | solution.py:339
  (16 shorter events, 0.1 us)
Async XLA Ops:
  6.5 78.0 %all-gather.12.cloned.1.call-start = ((), (), s32[]{:S(2)}) async-start(), calls=%async_computation.3 | async-start | bytes 3317760 | tf_op jit(solution)/shard_map/all_gather | solution.py:295
  7.8 79.0 %copy-start.3 = (f32[1280]{0:T(1024)S(1)}, f32[1280]{0:T(1024)}, u32[]{:S(2)}) copy-start(f32[1280]{0:T(1024)} %param.18) | copy-start | bytes 15364
  7.8 79.6 %copy-start.4 = (f32[20]{0:T(128)S(1)}, f32[20]{0:T(128)}, u32[]{:S(2)}) copy-start(f32[20]{0:T(128)} %param.17) | copy-start | bytes 244
  24.6 210.8 %all-gather.6.cloned.1.call-start = ((), (), s32[]{:S(2)}) async-start(), calls=%async_computation | async-start | bytes 7372800 | tf_op jit(solution)/shard_map/all_gather | solution.py:297
  25.9 24.4 %collective-permute-start.2 = (bf16[160,2560]{1,0:T(8,128)(2,1)S(1)}, bf16[160,2560]{1,0:T(8,128)(2,1)S(1)}, u32[]{:S(2)}, u32[]{:S(2)}) collective-permute-start(bf16[160,2560]{1,0:T(8,128)(2,1)S(1)} %constant_dynamic-slice_fusion), channel_id=1, source_target_pairs={{3,0},{0,1},{1,2},{2,3},{7,4},{4,5},{5,6},{6,7},{11,8},{8,9},{9,10... | collective-permute-start | bytes 2457608 | tf_op jit(solution)/shard_map/ppermute | solution.py:273
  29.0 55.5 %collective-permute-start.1 = (bf16[160,2560]{1,0:T(8,128)(2,1)S(1)}, bf16[160,2560]{1,0:T(8,128)(2,1)S(1)}, u32[]{:S(2)}, u32[]{:S(2)}) collective-permute-start(bf16[160,2560]{1,0:T(8,128)(2,1)S(1)} %constant_dynamic-slice_fusion), channel_id=1, source_target_pairs={{2,0},{3,1},{0,2},{1,3},{6,4},{7,5},{4,6},{5,7},{10,8},{11,9},{8,1... | collective-permute-start | bytes 2457608 | tf_op jit(solution)/shard_map/ppermute | solution.py:273
  31.6 52.9 %collective-permute-start = (bf16[160,2560]{1,0:T(8,128)(2,1)S(1)}, bf16[160,2560]{1,0:T(8,128)(2,1)S(1)}, u32[]{:S(2)}, u32[]{:S(2)}) collective-permute-start(bf16[160,2560]{1,0:T(8,128)(2,1)S(1)} %constant_dynamic-slice_fusion), channel_id=1, source_target_pairs={{1,0},{2,1},{3,2},{0,3},{5,4},{6,5},{7,6},{4,7},{9,8},{10,9},{11,1... | collective-permute-start | bytes 2457608 | tf_op jit(solution)/shard_map/ppermute | solution.py:273
  50.3 36.0 %copy-start = (bf16[160,2560]{1,0:T(8,128)(2,1)}, bf16[160,2560]{1,0:T(8,128)(2,1)S(1)}, u32[]{:S(2)}) copy-start(bf16[160,2560]{1,0:T(8,128)(2,1)S(1)} %collective-permute-done.2) | copy-start | bytes 2457604
  84.5 1.2 copy-start.1
  84.5 0.9 copy-start.2
  85.5 149.9 %all-gather.8.cloned.1.call-start = ((), (), s32[]{:S(2)}) async-start(), calls=%async_computation.1 | async-start | bytes 7372800 | tf_op jit(solution)/shard_map/all_gather | solution.py:297
  86.2 159.4 %all-gather.10.cloned.1.call-start = ((), (), s32[]{:S(2)}) async-start(), calls=%async_computation.2 | async-start | bytes 7372800 | tf_op jit(solution)/shard_map/all_gather | solution.py:297
Sparse Core Ops, SparseCore 0:
  24.8 34.0 all-gather.11
  85.6 63.2 all-gather.5
  150.8 46.4 all-gather.7
  199.1 46.4 all-gather.9
